TPU v7x, 8 devices: a whole 2x2x1 slice. The times are simulated.
8 devices in a mesh: rep: 1 (over z), dp: 8 (over x, y, core).
Axes of the slice: x: 2, y: 2, z: 1, core: 2. Of those that a mesh axis runs over, the one named last changes fastest.
Arguments:
- g_w_gate: bfloat16 [8, 2, 1024, 3200], P(('rep', 'dp'))
- g_w_up: bfloat16 [8, 2, 1024, 3200], P(('rep', 'dp'))
- g_w_down: bfloat16 [8, 2, 3200, 1024], P(('rep', 'dp'))
- w_gate: bfloat16 [2, 1024, 3200], replicated
- w_up: bfloat16 [2, 1024, 3200], replicated
- w_down: bfloat16 [2, 3200, 1024], replicated
- m_w_gate: float32 [2, 1024, 3200], P(None, 'dp')
- m_w_up: float32 [2, 1024, 3200], P(None, 'dp')
- m_w_down: float32 [2, 3200, 1024], P(None, 'dp')
- v_w_gate: float32 [2, 1024, 3200], P(None, 'dp')
- v_w_up: float32 [2, 1024, 3200], P(None, 'dp')
- v_w_down: float32 [2, 3200, 1024], P(None, 'dp')
Outputs:
- output 1: bfloat16 [2, 1024, 3200], P('rep')
- output 2: bfloat16 [2, 1024, 3200], P('rep')
- output 3: bfloat16 [2, 3200, 1024], P('rep')
- output 4: float32 [2, 1024, 3200], P('rep', 'dp')
- output 5: float32 [2, 1024, 3200], P('rep', 'dp')
- output 6: float32 [2, 3200, 1024], P('rep', 'dp')
- output 7: float32 [2, 1024, 3200], P('rep', 'dp')
- output 8: float32 [2, 1024, 3200], P('rep', 'dp')
- output 9: float32 [2, 3200, 1024], P('rep', 'dp')
All inputs are finite; a program needn't handle non-finite values.
Results may differ from a plain program's by a relative error of at most 0.022.
Values are sent between devices in bfloat16 or wider.
A program may use at most 2 GiB of HBM per device.

v0:
```python
import jax
import jax.numpy as jnp
from jax import lax
from jax.sharding import PartitionSpec as P


def adamw(w, m, v, g):
    m = 0.9 * m + 0.1 * g
    v = 0.95 * v + 0.05 * g * g
    step = m * lax.rsqrt(v + 1e-8) + 0.1 * w
    return (w - 0.02 * step).astype(jnp.bfloat16), m, v


def clipped(gradients, sum_of_squares, count):
    factor = jnp.minimum(1.0, 0.5 * lax.rsqrt(sum_of_squares / count + 1e-30))
    return [g * factor for g in gradients]


def solution(mesh):
    def step(*arrays):
        terms, weights, m, v = (arrays[i : i + 3] for i in (0, 3, 6, 9))
        gradients = [lax.psum_scatter(t[0], "dp", scatter_dimension=1, tiled=True).astype(jnp.float32) for t in terms]
        squares = lax.psum(sum(jnp.sum(g * g) for g in gradients), "dp")
        gradients = clipped(gradients, squares, lax.psum(1, "dp") * sum(g.size for g in gradients))
        me = lax.axis_index("dp")
        own = [lax.dynamic_slice_in_dim(w, me * one.shape[1], one.shape[1], 1).astype(jnp.float32) for w, one in zip(weights, m, strict=True)]
        new = [adamw(w, m, v, g) for w, m, v, g in zip(own, m, v, gradients, strict=True)]
        whole = [lax.all_gather(one[0], "dp", axis=1, tiled=True) for one in new]
        return (*whole, *(one[1] for one in new), *(one[2] for one in new))

    all_of, cut = P(None, None, None), P(None, "dp", None)
    return jax.shard_map(
        step,
        mesh=mesh,
        in_specs=(P(("rep", "dp"), None, None, None),) * 3 + (all_of,) * 3 + (cut,) * 6,
        out_specs=(P("rep", None, None),) * 3 + (P("rep", "dp", None),) * 6,
        check_vma=False,
    )
```

profile of v0, /device:TPU:0, one launch (start us, length us, event | category | flops | bytes accessed | tf_op | source)
XLA Modules:
  0.0 559.3 jit_solution(9752428845764022567)
XLA Ops:
  7.2 0.0 reduce-scatter.4.cloned.1.call-start
  7.2 0.7 reduce-scatter.4.cloned.1.call-update
  7.9 0.0 reduce-scatter.6.cloned.1.call-start
  8.0 0.7 reduce-scatter.6.cloned.1.call-update
  8.7 0.0 reduce-scatter.8.cloned.1.call-start
  8.7 0.7 reduce-scatter.8.cloned.1.call-update
  9.4 0.0 all-gather.8.cloned.1.call-start
  9.4 91.1 %reduce-scatter.4.cloned.1.call-done = bf16[2,128,3200]{2,1,0:T(8,128)(2,1)} async-done(((bf16[2,1024,3200]{2,1,0:T(8,128)(2,1)}), bf16[2,128,3200]{2,1,0:T(8,128)(2,1)}) %reduce-scatter.4.cloned.1.call-update) | async-done | bytes 1638416 | tf_op jit(solution)/shard_map/reduce_scatter | solution.py:22
  100.5 2.9 fusion.9
  103.4 86.9 %reduce-scatter.6.cloned.1.call-done = bf16[2,128,3200]{2,1,0:T(8,128)(2,1)} async-done(((bf16[2,1024,3200]{2,1,0:T(8,128)(2,1)}), bf16[2,128,3200]{2,1,0:T(8,128)(2,1)}) %reduce-scatter.6.cloned.1.call-update) | async-done | bytes 1638416 | tf_op jit(solution)/shard_map/reduce_scatter | solution.py:22
  190.3 2.9 fusion.10
  194.5 85.6 %reduce-scatter.8.cloned.1.call-done = bf16[2,400,1024]{2,1,0:T(8,128)(2,1)} async-done(((bf16[2,3200,1024]{2,1,0:T(8,128)(2,1)}), bf16[2,400,1024]{2,1,0:T(8,128)(2,1)}) %reduce-scatter.8.cloned.1.call-update) | async-done | bytes 1638416 | tf_op jit(solution)/shard_map/reduce_scatter | solution.py:22
  280.1 2.9 fusion.11
  283.6 22.2 %psum.7 = f32[]{:T(128)} all-reduce(f32[]{:T(128)S(6)} %add.65), channel_id=1, replica_groups=mesh['rep'=1,'dp'=8] {'dp'}, use_global_device_ids=true, to_apply=%region_6.0 | all-reduce | flops 1 | bytes 8 | tf_op jit(solution)/shard_map/psum | solution.py:23
  306.5 0.0 copy-start.2
  306.6 6.5 %fusion.17 = (bf16[2,400,1024]{2,1,0:T(8,128)(2,1)}, f32[2,400,1024]{2,1,0:T(8,128)}, f32[2,400,1024]{2,1,0:T(8,128)}) fusion(bf16[2,3200,1024]{2,1,0:T(8,128)(2,1)} %param.17, s32[]{:T(128)S(6)} %select_n.8, f32[]{:T(128)S(6)} %min_shard_map.3, bf16[2,400,1024]{2,1,0:T(8,128)(2,1)} %reduce-scatter.8.cloned.1.call-done, f32[2,400,1024]{2,1,0:T(8,128)} %param.23, ...), kind=kLoop, calls=%fused_computation.32 | loop fusion | flops 13926400 | bytes 18022408 | tf_op jit(solution)/shard_map/convert_element_type | solution.py:11
  313.1 0.0 all-gather.8.cloned.1.call-update
  313.1 0.0 all-gather.4.cloned.1.call-start
  313.1 0.0 copy-done.2
  313.1 0.0 copy-start.1
  313.2 6.1 %fusion.8 = (bf16[2,128,3200]{2,1,0:T(8,128)(2,1)}, f32[2,128,3200]{2,1,0:T(8,128)}, f32[2,128,3200]{2,1,0:T(8,128)}) fusion(bf16[2,1024,3200]{2,1,0:T(8,128)(2,1)} %param.15, s32[]{:T(128)S(6)} %select_n.7, f32[]{:T(128)S(6)} %min_shard_map.3, bf16[2,128,3200]{2,1,0:T(8,128)(2,1)S(1)} %copy-done.2, f32[2,128,3200]{2,1,0:T(8,128)} %param.21, ...), kind=kLoop, calls=%fused_computation.23 | loop fusion | flops 13926400 | bytes 18022408 | tf_op jit(solution)/shard_map/convert_element_type | solution.py:11
  319.3 0.0 all-gather.4.cloned.1.call-update
  319.3 0.0 all-gather.6.cloned.1.call-start
  319.3 0.0 copy-done.1
  319.3 7.5 %fusion.14 = (bf16[2,128,3200]{2,1,0:T(8,128)(2,1)}, f32[2,128,3200]{2,1,0:T(8,128)}, f32[2,128,3200]{2,1,0:T(8,128)}) fusion(bf16[2,1024,3200]{2,1,0:T(8,128)(2,1)} %param.16, s32[]{:T(128)S(6)} %select_n.7, f32[]{:T(128)S(6)} %min_shard_map.3, bf16[2,128,3200]{2,1,0:T(8,128)(2,1)S(1)} %copy-done.1, f32[2,128,3200]{2,1,0:T(8,128)} %param.22, ...), kind=kLoop, calls=%fused_computation.29 | loop fusion | flops 13926400 | bytes 18022408 | tf_op jit(solution)/shard_map/convert_element_type | solution.py:11
  326.8 0.0 all-gather.6.cloned.1.call-update
  326.9 56.9 %all-gather.8.cloned.1.call-done = bf16[2,3200,1024]{2,1,0:T(8,128)(2,1)} async-done(((bf16[2,400,1024]{2,1,0:T(8,128)(2,1)}), bf16[2,3200,1024]{2,1,0:T(8,128)(2,1)}) %all-gather.8.cloned.1.call-update) | async-done | bytes 13107216 | tf_op jit(solution)/shard_map/all_gather | solution.py:28
  383.8 70.9 %all-gather.4.cloned.1.call-done = bf16[2,1024,3200]{2,1,0:T(8,128)(2,1)} async-done(((bf16[2,128,3200]{2,1,0:T(8,128)(2,1)}), bf16[2,1024,3200]{2,1,0:T(8,128)(2,1)}) %all-gather.4.cloned.1.call-update) | async-done | bytes 13107216 | tf_op jit(solution)/shard_map/all_gather | solution.py:28
  454.7 70.9 %all-gather.6.cloned.1.call-done = bf16[2,1024,3200]{2,1,0:T(8,128)(2,1)} async-done(((bf16[2,128,3200]{2,1,0:T(8,128)(2,1)}), bf16[2,1024,3200]{2,1,0:T(8,128)(2,1)}) %all-gather.6.cloned.1.call-update) | async-done | bytes 13107216 | tf_op jit(solution)/shard_map/all_gather | solution.py:28
  525.7 0.0 copy-start
  525.7 0.0 slice-start
  525.7 0.0 slice-start.1
  525.7 0.0 slice-start.2
  525.7 12.7 %copy.24 = bf16[2,1024,3200]{2,1,0:T(8,128)(2,1)} copy(bf16[2,1024,3200]{2,1,0:T(8,128)(2,1)} %all-gather.4.cloned.1.call-done) | data formatting | bytes 26214400
  538.4 0.0 copy-done
  538.4 0.0 slice-start.3
  538.4 6.6 %copy.25 = bf16[2,1024,3200]{2,1,0:T(8,128)(2,1)} copy(bf16[2,1024,3200]{2,1,0:T(8,128)(2,1)S(1)} %copy-done) | data formatting | bytes 26214400
  545.0 0.0 slice-done
  545.0 1.2 slice-done.1
  546.2 1.2 slice-done.2
  547.4 0.1 slice-done.3
  547.5 4.9 copy.26
  (1 shorter events, 0.0 us)
Async XLA Ops:
  7.2 93.4 %reduce-scatter.4.cloned.1.call-start = ((), (), s32[]{:S(2)}) async-start(), calls=%async_computation.3 | async-start | bytes 14745600 | tf_op jit(solution)/shard_map/reduce_scatter | solution.py:22
  7.9 182.4 %reduce-scatter.6.cloned.1.call-start = ((), (), s32[]{:S(2)}) async-start(), calls=%async_computation.4 | async-start | bytes 14745600 | tf_op jit(solution)/shard_map/reduce_scatter | solution.py:22
  8.7 271.4 %reduce-scatter.8.cloned.1.call-start = ((), (), s32[]{:S(2)}) async-start(), calls=%async_computation.5 | async-start | bytes 14745600 | tf_op jit(solution)/shard_map/reduce_scatter | solution.py:22
  9.4 374.4 %all-gather.8.cloned.1.call-start = ((), (), s32[]{:S(2)}) async-start(), calls=%async_computation.8 | async-start | bytes 14745600 | tf_op jit(solution)/shard_map/all_gather | solution.py:28
  306.5 6.6 %copy-start.2 = (bf16[2,128,3200]{2,1,0:T(8,128)(2,1)S(1)}, bf16[2,128,3200]{2,1,0:T(8,128)(2,1)}, u32[]{:S(2)}) copy-start(bf16[2,128,3200]{2,1,0:T(8,128)(2,1)} %reduce-scatter.4.cloned.1.call-done) | copy-start | bytes 4915204
  313.1 141.7 %all-gather.4.cloned.1.call-start = ((), (), s32[]{:S(2)}) async-start(), calls=%async_computation.6 | async-start | bytes 14745600 | tf_op jit(solution)/shard_map/all_gather | solution.py:28
  313.1 6.2 %copy-start.1 = (bf16[2,128,3200]{2,1,0:T(8,128)(2,1)S(1)}, bf16[2,128,3200]{2,1,0:T(8,128)(2,1)}, u32[]{:S(2)}) copy-start(bf16[2,128,3200]{2,1,0:T(8,128)(2,1)} %reduce-scatter.6.cloned.1.call-done) | copy-start | bytes 4915204
  319.3 206.4 %all-gather.6.cloned.1.call-start = ((), (), s32[]{:S(2)}) async-start(), calls=%async_computation.7 | async-start | bytes 14745600 | tf_op jit(solution)/shard_map/all_gather | solution.py:28
  525.7 12.7 %copy-start = (bf16[2,1024,3200]{2,1,0:T(8,128)(2,1)S(1)}, bf16[2,1024,3200]{2,1,0:T(8,128)(2,1)}, u32[]{:S(2)}) copy-start(bf16[2,1024,3200]{2,1,0:T(8,128)(2,1)} %all-gather.6.cloned.1.call-done) | copy-start | bytes 39321604
  525.7 19.4 %slice-start = ((s8[13107200]{0:T(1024)(128)(4,1)}), s8[4194304]{0:T(1024)(128)(4,1)S(1)}, s32[]{:S(2)}) async-start(s8[13107200]{0:T(1024)(128)(4,1)} %bitcast.6), calls=%async_computation.9 | async-start | bytes 8388608
  525.7 20.5 %slice-start.1 = ((s8[13107200]{0:T(1024)(128)(4,1)}), s8[4194304]{0:T(1024)(128)(4,1)S(1)}, s32[]{:S(2)}) async-start(s8[13107200]{0:T(1024)(128)(4,1)} %bitcast.6), calls=%async_computation.10 | async-start | bytes 8388608
  525.7 21.7 %slice-start.2 = ((s8[13107200]{0:T(1024)(128)(4,1)}), s8[4194304]{0:T(1024)(128)(4,1)S(1)}, s32[]{:S(2)}) async-start(s8[13107200]{0:T(1024)(128)(4,1)} %bitcast.6), calls=%async_computation.11 | async-start | bytes 8388608
  538.4 9.1 %slice-start.3 = ((s8[13107200]{0:T(1024)(128)(4,1)}), s8[524288]{0:T(1024)(128)(4,1)S(1)}, s32[]{:S(2)}) async-start(s8[13107200]{0:T(1024)(128)(4,1)} %bitcast.6), calls=%async_computation.12 | async-start | bytes 1048576
Sparse Core Ops, SparseCore 0:
  11.5 89.0 reduce-scatter.3
  104.1 86.2 reduce-scatter.5
  193.8 86.2 reduce-scatter.7
  313.2 70.5 all-gather.7
  386.1 68.6 all-gather.3
  457.0 68.6 all-gather.5
where the time goes:
time: 560 us; the launch traced here: 559 us
  waiting for transfers between devices  465 us (83%)
  other arithmetic  28.7 us (5%)
  local copies, waits for them, and re-layouts  26.8 us (5%)
  blocking collectives  22.2 us (4%)
  between operations  16.8 us (3%)
    reduce_scatter x3, waiting for transfers between devices, step(): lax.psum_scatter(t[0], 'dp', scatter_dimension=1, tiled=True)  264 us
    all_gather x3, waiting for transfers between devices, step(): whole = [lax.all_gather(one[0], 'dp', axis=1, tiled=True) for one in new]  199 us
    unnamed x17, local copies, waits for them, and re-layouts  26.8 us
    psum x1, blocking collectives, step(): squares = lax.psum(sum((jnp.sum(g * g) for g in gradients)), 'dp')  22.2 us
    convert_element_type x3, other arithmetic, adamw(): return ((w - 0.02 * step).astype(jnp.bfloat16), m, v)  20.1 us
  transfers between devices with their start and end apart: 6, of which 6 were waited for; matrix products, arithmetic and copies ran while one was open for 3% of the time, Pallas kernels for 0%

commit v1 on v0

v1 whole, which is shorter than its diff:
```python
import functools

import jax
import jax.numpy as jnp
from jax import lax
from jax.experimental import pallas as pl
from jax.experimental.pallas import tpu as pltpu
from jax.sharding import PartitionSpec as P


D, FF, LAYERS, N = 1024, 3200, 2, 8
COUNT = 3 * LAYERS * D * FF
BLOCKS = ((0, 0), (0, 1), (1, 0), (1, 1), (2, 0), (2, 1))
LAST = 96
FIRST = 32
AHEAD = 6
RING = 4
VMEM = 67043328
BF, FL = jnp.bfloat16, jnp.float32
HALVES = (0, 1)
LANES, PACK = 128, 16
TILE = (8, LANES)
WIDE, TALL, HALF_WIDE, HALF_TALL = (128, 3200), (400, 1024), (64, 3200), (208, 1024)
DEPTH = 8
WINDOW = 2


def rows_of(b):
    return (WIDE if b < 4 else TALL)[0]


def half(b, h):
    rows = rows_of(b)
    split = rows // 2 if b < 4 else rows // 2 + (8 if b == 4 else -8)
    return (split, rows - split) if h else (0, split)


def tiles(b, num, body, carry):
    full, width = (WIDE[1], 640) if b < 4 else (TALL[1], 512)

    def one(i, carry):
        at = pl.ds(pl.multiple_of(i * PACK, PACK), PACK)
        for first in range(0, full, width):
            carry = body(at, pl.ds(first, width), width, carry)
        return carry

    return lax.fori_loop(0, num // PACK, one, carry)


def fold(x):
    return sum(x[:, k:k + LANES] for k in range(0, x.shape[1], LANES))


def f32(x):
    return x.astype(FL)


def passed_on(h):
    n4, n5, (l4, l5) = half(4, h)[1], half(5, h)[1], (half(4, h)[0], half(5, h)[0])
    lo, num = half(0, h)
    table = [(0, 0, 0, lo, FIRST), (1, 0, 0, lo + FIRST, num - FIRST)]
    table += [(1, num * b - FIRST, b, half(b, h)[0], num) for b in (1, 2, 3)]
    return table + [(2, 0, 4, l4, n4), (2, n4, 5, l5, n5 - LAST), (3, 0, 5, l5 + n5 - LAST, LAST)]


def kernel(gg, gu, gd, wg, wu, wd, mg, mu, md, vg, vu, vd,
           og, ou, od, qg, qu, qd, fac_out, *rest):
    pass_x, pass_y, land_x, land_y, \
        own_a, own_b, part_a, part_b, rec_a, rec_b, mv_a, mv_b, ws_a, ws_b, sq, nrm, \
        fac, load_sem, d2d_send, d2d_recv, link_send, link_recv, nrm_send, nrm_recv, \
        wmv_sem, out_sem, g_sem, fac_sem = (rest[0:4], rest[4:8], *rest[8:])
    grads, weights, ms, vs, outs, qs = (gg, gu, gd), (wg, wu, wd), (mg, mu, md), (vg, vu, vd), (og, ou, od), (qg, qu, qd)
    me = lax.axis_index("dp")
    x, y, c = lax.div(me, 4), lax.rem(lax.div(me, 2), 2), lax.rem(me, 2)

    def device(r, other=0):
        cx, cy = lax.rem(x + r // 2, 2), lax.rem(y + r % 2, 2)
        return cx * 4 + cy * 2 + (1 - c if other else c)

    def to(index):
        return dict(device_id={"dp": index}, device_id_type=pl.DeviceIdType.MESH)

    across = (device(2), device(1))
    partner = device(0, 1)

    def own(p, r):
        b, _, lo, num = p
        return own_a.at[b, r, pl.ds(lo, num)] if b < 4 else own_b.at[b - 4, r, pl.ds(lo, num)]

    def part(p, r):
        b, _, lo, num = p
        return part_a.at[b, r, pl.ds(lo, num)] if b < 4 else part_b.at[b - 4, r, pl.ds(lo, num)]

    def rec(p, k):
        b, h, lo, num = p
        at = pl.ds(lo - half(b, h)[0], num)
        return rec_a.at[b, h, k, at] if b < 4 else rec_b.at[b - 4, h, k, at]

    def span(ref, p, dev, lead=()):
        b, _, lo, num = p
        w, layer = BLOCKS[b]
        return ref[w].at[(*lead, layer, pl.ds(pl.multiple_of(dev * rows_of(b) + lo, PACK), num))]

    def mine(ref, p):
        b, _, lo, num = p
        return ref[BLOCKS[b][0]].at[BLOCKS[b][1], pl.ds(lo, num)]

    def cut(b, h, *firsts):
        lo, num = half(b, h)
        found = []
        for n in (*firsts, num - sum(firsts)):
            found.append((b, h, lo, n))
            lo += n
        return found

    barrier = pltpu.get_barrier_semaphore()
    for k in range(1, N):
        pl.semaphore_signal(barrier, inc=1, **to(lax.rem(me + k, N)))

    def chip(kind, h):
        return {"S1": 3, "S2": (2, 1)[h], "R": (1, 2)[h], "G": 0}[kind]

    pieces = {}
    for h in HALVES:
        pieces["S1", h] = [p for b in range(6) for p in (cut(b, h, 16) if b == 0 else cut(b, h))]
        pieces["S2", h] = [p for b in range(6) for p in cut(b, h)]
        pieces["R", h] = pieces["G", h] = [p for b in range(6) for p in (cut(b, h, half(b, h)[1] - 48) if b == 5 else cut(b, h))]
    pairs = {kind: list(zip(pieces[kind, 0], pieces[kind, 1], strict=True)) for kind in ("S1", "S2", "R", "G")}
    turns = [("S1", pair) for pair in pairs["S1"]] + [("S2", pair) for pair in pairs["S2"]]
    for n in range(len(pairs["R"]) + 2):
        turns += [("R", pair) for pair in pairs["R"][n:n + 1]] + [("G", pair) for pair in pairs["G"][n - 2:n - 1] if n >= 2]
    units = [(p[0], chip("S1", 0), *p[2:]) for pair in pairs["S1"][:2] for p in pair]
    units += [(b, chip("S1", 0), 0, rows_of(b)) for b in range(1, 6)]
    units += [(b, chip("S2", h), 0, rows_of(b)) for b in range(6) for h in HALVES]
    units += [(b, 0, 0, rows_of(b)) for b in range(6)]
    loads, d2ds, here = {}, {}, set()

    def fetch_own(i):
        b, r, lo, num = units[i]
        p = (b, None, lo, num)
        loads[i] = pltpu.make_async_copy(span(grads, p, device(r), (0,)), own(p, r), load_sem.at[i % AHEAD])
        loads[i].start()

    def fetch_part(i):
        b, r, lo, num = units[i]
        p = (b, None, lo, num)
        d2ds[i] = pltpu.make_async_remote_copy(
            span(grads, p, device(r, 1), (0,)), part(p, r), d2d_send.at[i % AHEAD], d2d_recv.at[i], **to(partner))
        d2ds[i].start()

    for i in range(AHEAD):
        fetch_own(i)
    pl.semaphore_wait(barrier, N - 1)
    for i in range(AHEAD):
        fetch_part(i)

    def ready(p, r):
        for i, (b, chip_, lo, num) in enumerate(units):
            if (b, chip_) == (p[0], r) and lo <= p[2] and p[2] + p[3] <= lo + num and i not in here:
                here.add(i)
                loads[i].wait()
                d2ds[i].wait()
                if i + AHEAD < len(units):
                    fetch_own(i + AHEAD)
                    fetch_part(i + AHEAD)

    def add(p, r, terms, squares=False):
        b, _, _, num = p
        target = own(p, r)

        def body(at, cols, width, carry):
            total = f32(target[at, cols])
            for t in terms:
                total = total + f32(t[at, cols])
            rounded = total.astype(BF)
            target[at, cols] = rounded
            return carry + f32(rounded) * f32(rounded) if squares else carry

        width = 640 if b < 4 else 512
        done = tiles(b, num, body, jnp.zeros((PACK, width), FL) if squares else 0)
        if squares:
            sq[...] += fold(done)

    links, arrivals = [[], []], [{}, {}]

    def send(d, p, r, k):
        i = len(links[d])
        if i >= WINDOW:
            links[d][i - WINDOW].wait_send()
        one = pltpu.make_async_remote_copy(own(p, r), rec(p, k), link_send.at[d, i % WINDOW], link_recv.at[d, i], **to(across[d]))
        one.start()
        links[d].append(one)
        arrivals[d][p, k] = one

    sq[...] = jnp.zeros_like(sq)
    for kind, pair in turns:
        if kind in ("S1", "S2"):
            for h, p in enumerate(pair):
                r = chip(kind, h)
                ready(p, r)
                add(p, r, [part(p, r)])
                send(h, p, r, int(kind == "S2"))

    def slot(b, h, lo=0, num=None):
        at = pl.ds(lo, half(b, h)[1] if num is None else num)
        if b < 4:
            return mv_a.at[h, 0, at], mv_a.at[h, 1, at], ws_a.at[h, at]
        return mv_b.at[h, 0, at], mv_b.at[h, 1, at], ws_b.at[h, at]

    states = {}

    def fetch_state(b, h):
        m, v, w = slot(b, h)
        p = cut(b, h)[0]
        states[b, h] = [
            pltpu.make_async_copy(mine(ms, p), m, wmv_sem.at[b // 4, h, 0]),
            pltpu.make_async_copy(mine(vs, p), v, wmv_sem.at[b // 4, h, 1]),
            pltpu.make_async_copy(span(weights, p, me), w, wmv_sem.at[b // 4, h, 2]),
        ]
        for one in states[b, h]:
            one.start()

    for b in (0, 4):
        for h in HALVES:
            fetch_state(b, h)

    keep, waited = {}, set()

    def kept(b):
        if b not in waited:
            waited.add(b)
            keep[b].wait()

    def finish(pair):
        for h, p in enumerate(pair):
            ready(p, 0)
            if (cut(p[0], h)[0], 1) not in waited:
                waited.add((cut(p[0], h)[0], 1))
                arrivals[h][cut(p[0], h)[0], 1].wait_recv()
            arrivals[1 - h][p, 2].wait_recv()
            add(p, 0, [part(p, 0), rec(p, 1), rec(p, 2)], squares=True)
        if pair is pairs["G"][-1] or pair[0][0] != pairs["G"][pairs["G"].index(pair) + 1][0][0]:
            b = pair[0][0]
            if b >= RING:
                kept(b - RING)
            p = (b, None, 0, rows_of(b))
            keep[b] = pltpu.make_async_copy(own(p, 0), mine(qs, p), g_sem.at[b % RING])
            keep[b].start()

    for kind, pair in turns:
        if kind == "G":
            finish(pair)
        elif kind == "R":
            for h, p in enumerate(pair):
                r = chip("R", h)
                ready(p, r)
                for q in pieces["S1", h]:
                    if q[0] == p[0] and (q, 0) not in waited:
                        waited.add((q, 0))
                        arrivals[h][q, 0].wait_recv()
                add(p, r, [part(p, r), rec(p, 0)])
                send(1 - h, p, r, 2)

    nrm[me] = sq[0:8] + sq[8:16]
    sums = []
    for k in range(1, N):
        other = lax.rem(me + k, N)
        one = pltpu.make_async_remote_copy(nrm.at[me], nrm.at[me], nrm_send.at[k], nrm_recv.at[me], **to(other))
        one.start()
        sums.append(one)
    for k in range(1, N):
        other = lax.rem(me + k, N)
        pltpu.make_async_remote_copy(nrm.at[other], nrm.at[other], nrm_send.at[k], nrm_recv.at[other], **to(other)).wait_recv()
    total = nrm[0]
    for k in range(1, N):
        total = total + nrm[k]
    total = jnp.full(TILE, jnp.sum(total), FL)
    fac[...] = jnp.minimum(1.0, 0.5 * lax.rsqrt(total / COUNT + 1e-30))
    fac_copy = pltpu.make_async_copy(fac, fac_out, fac_sem.at[0])
    fac_copy.start()

    def adamw(p):
        b, h, lo, num = p
        if (b, h) not in stepped:
            stepped.add((b, h))
            for one in states[b, h]:
                one.wait()
            kept(b)
        m_ref, v_ref, w_ref = slot(b, h, lo - half(b, h)[0], num)
        target = own(p, 0)

        def body(at, cols, width, carry):
            g = f32(target[at, cols]) * jnp.broadcast_to(fac[0:1, 0:1], (PACK, width))
            m = 0.9 * m_ref[at, cols] + 0.1 * g
            v = 0.95 * v_ref[at, cols] + 0.05 * g * g
            w = f32(w_ref[at, cols])
            step = m * lax.rsqrt(v + 1e-8) + 0.1 * w
            target[at, cols] = (w - 0.02 * step).astype(BF)
            return carry

        tiles(b, num, body, 0)

    stepped = set()
    gats, moves, locals_ = [[], []], [], []
    passes, lands = (pass_x, pass_y), (land_x, land_y)

    def gather_send(d, src, dst, note):
        i = len(gats[d])
        (gats[d][i - WINDOW][0] if i >= WINDOW else links[d][i - WINDOW]).wait_send()
        one = pltpu.make_async_remote_copy(src, dst, link_send.at[d, i % WINDOW], link_recv.at[d, i], **to(across[d]))
        one.start()
        gats[d].append((one, note))

    def hand_over(src, p, dev):
        i = len(moves)
        if i >= AHEAD:
            moves[i - AHEAD].wait_send()
        one = pltpu.make_async_remote_copy(src, span(outs, p, dev), d2d_send.at[i % AHEAD], d2d_recv.at[i], **to(partner))
        one.start()
        moves.append(one)

    def arrived(d, i):
        one, note = gats[d][i]
        one.wait_recv()
        if note is not None:
            ref, p = note
            hand_over(ref, p, across[d])

    def settle_own(b):
        p = (b, None, 0, rows_of(b))
        hand_over(own(p, 0), p, me)
        if b >= RING:
            locals_[b - RING].wait()
        one = pltpu.make_async_copy(own(p, 0), span(outs, p, me), out_sem.at[b % RING])
        one.start()
        locals_.append(one)

    tables = [[(a, row, (b, d, lo, num)) for a, row, b, lo, num in passed_on(d)] for d in HALVES]
    count = len(tables[0])
    for n in range(count + 6):
        for d in HALVES:
            if n < count:
                a, row, p = tables[d][n]
                adamw(p)
                b = p[0]
                if b not in [q[2][0] for q in tables[d][n + 1:]] and b not in (3, 5):
                    fetch_state(b + 1, d)
                ref = passes[d][a].at[pl.ds(row, p[3])]
                gather_send(d, own(p, 0), ref, (ref, p))
            else:
                p = cut(n - count, 1 - d)[0]
                gather_send(d, own(p, 0), span(outs, p, me), (span(outs, p, across[d]), p))
        if n < count and b not in [q[2][0] for q in tables[0][n + 1:]]:
            settle_own(b)
        if n >= WINDOW:
            for d in HALVES:
                arrived(d, n - WINDOW)
    for d in HALVES:
        gather_send(d, passes[1 - d][0], lands[1 - d], None)
    for n in range(count + 4, count + 7):
        for d in HALVES:
            arrived(d, n)

    for d in HALVES:
        for one, _ in gats[d][-WINDOW:]:
            one.wait_send()
    for one in sums:
        one.wait_send()
    for one in locals_[-RING:]:
        one.wait()
    for i, one in enumerate(moves):
        one.wait_recv()
        if i >= len(moves) - AHEAD:
            one.wait_send()
    fac_copy.wait()


ONWARD = [(FIRST, FF), (2 * WIDE[0] - FIRST, FF), (TALL[0] - LAST, D), (LAST, D)]


def communicate(*arrays):
    any_, dma = pl.BlockSpec(memory_space=pl.ANY), pltpu.SemaphoreType.DMA
    wide, tall = [(LAYERS, D, FF)] * 2 + [(LAYERS, FF, D)], [(LAYERS, *WIDE)] * 2 + [(LAYERS, *TALL)]
    shapes = [jax.ShapeDtypeStruct(s, BF) for s in wide + tall] + [jax.ShapeDtypeStruct(TILE, FL)]
    shapes += [jax.ShapeDtypeStruct(s, BF) for s in ONWARD + ONWARD + ONWARD[:1] * 2]
    return pl.pallas_call(
        kernel,
        out_shape=shapes,
        in_specs=[any_] * len(arrays),
        out_specs=[any_] * len(shapes),
        scratch_shapes=[
            *(pltpu.VMEM((4, 4, *WIDE), BF), pltpu.VMEM((2, 4, *TALL), BF)) * 2,
            pltpu.VMEM((4, 2, 3, *HALF_WIDE), BF), pltpu.VMEM((2, 2, 3, *HALF_TALL), BF),
            pltpu.VMEM((2, 2, *HALF_WIDE), FL), pltpu.VMEM((2, 2, *HALF_TALL), FL),
            pltpu.VMEM((2, *HALF_WIDE), BF), pltpu.VMEM((2, *HALF_TALL), BF),
            pltpu.VMEM((PACK, LANES), FL), pltpu.VMEM((N, *TILE), FL), pltpu.VMEM(TILE, FL),
            dma((AHEAD,)), dma((AHEAD,)), dma((34,)), dma((2, WINDOW)), dma((2, 20)), dma((N,)), dma((N,)),
            dma((2, 2, 3)), dma((RING,)), dma((RING,)), dma((1,)),
        ],
        compiler_params=pltpu.CompilerParams(collective_id=0, has_side_effects=True, vmem_limit_bytes=VMEM),
    )(*arrays)


def stream(pieces, slots, sem, depth):
    n, count = len(pieces), slots.shape[0]
    loads = [pltpu.make_async_copy(src, slots.at[i % count, pl.ds(0, src.shape[0])], sem.at[i % count]) for i, (src, _) in enumerate(pieces)]
    stores = [pltpu.make_async_copy(slots.at[i % count, pl.ds(0, dst.shape[0])], dst, sem.at[i % count]) for i, (_, dst) in enumerate(pieces)]
    for i in range(n + depth):
        if i < n:
            if i >= count:
                stores[i - count].wait()
            loads[i].start()
        if i >= depth:
            loads[i - depth].wait()
            stores[i - depth].start()
    for one in stores[max(0, n - count):]:
        one.wait()


def device_of(r, other):
    me = lax.axis_index("dp")
    x, y, c = lax.div(me, 4), lax.rem(lax.div(me, 2), 2), lax.rem(me, 2)
    return lax.rem(x + r // 2, 2) * 4 + lax.rem(y + r % 2, 2) * 2 + (1 - c if other else c)


def rows(ref, b, dev, lo, num):
    return ref.at[BLOCKS[b][1], pl.ds(pl.multiple_of(dev * rows_of(b) + lo, PACK), num)]


def settle_kernel(done, moments, *refs):
    refs = list(refs)
    take = lambda n: [refs.pop(0) for _ in range(n)]
    tmps, passed = dict(zip(done, take(len(done)))), (take(4), take(4))
    qs, fac, ms, vs = (take(3), take(1)[0], take(3), take(3)) if moments else (None,) * 4
    outs = dict(zip(done, take(len(done))))
    new_ms, new_vs = (take(3), take(3)) if moments else (None,) * 2
    wide, tall, mv_a, mv_b, g_a, g_b, factor, c_sem, m_sem, f_sem = refs
    if moments:
        get = pltpu.make_async_copy(fac, factor, f_sem.at[0])
        get.start()

    copies, steps = [], []
    for b in range(6):
        w, _ = BLOCKS[b]
        if moments:
            steps += [(b, h) for h in HALVES]
        if w not in done:
            continue
        for r in (0, 1, 2):
            for other in HALVES:
                dev = device_of(r, other)
                if r == 0 or other:
                    copies.append((b, rows(tmps[w], b, dev, 0, rows_of(b)), rows(outs[w], b, dev, 0, rows_of(b))))
                    continue
                for h in HALVES:
                    if h == r - 1:
                        lo, num = half(b, h)
                        copies.append((b, rows(tmps[w], b, dev, lo, num), rows(outs[w], b, dev, lo, num)))
                    else:
                        copies += [
                            (b, passed[h][a].at[pl.ds(row, num)], rows(outs[w], b, dev, lo, num))
                            for a, row, c, lo, num in passed_on(h) if c == b
                        ]

    loads, stores, work, users = [], [], [], []
    counts = {}

    def place(kind, slots):
        k = counts.get(kind, 0)
        counts[kind] = k + 1
        return k % slots

    def copy_task(b, src, dst):
        kind, ref, base = ("wide", wide, 0) if b < 4 else ("tall", tall, wide.shape[0])
        k = place(kind, ref.shape[0])
        mid = ref.at[k, pl.ds(0, src.shape[0])]
        loads.append([pltpu.make_async_copy(src, mid, c_sem.at[base + k])])
        stores.append([pltpu.make_async_copy(mid, dst, c_sem.at[base + k])])
        work.append(None)
        users.append((kind, k))

    def moment_task(b, h):
        kind, mv, gs, base = ("a", mv_a, g_a, 0) if b < 4 else ("b", mv_b, g_b, mv_a.shape[0])
        k = place(kind, mv.shape[0])
        w, layer = BLOCKS[b]
        lo, num = half(b, h)
        m, v, g = mv.at[k, 0, pl.ds(0, num)], mv.at[k, 1, pl.ds(0, num)], gs.at[k, pl.ds(0, num)]

        def at(refs_):
            return refs_[w].at[layer, pl.ds(lo, num)]

        loads.append([pltpu.make_async_copy(at(x), y, m_sem.at[i, base + k]) for i, (x, y) in enumerate(((ms, m), (vs, v), (qs, g)))])
        stores.append([pltpu.make_async_copy(y, at(x), m_sem.at[i, base + k]) for i, (x, y) in enumerate(((new_ms, m), (new_vs, v)))])
        users.append((kind, k))

        def compute():
            def body(at, cols, width, carry):
                one = f32(g[at, cols]) * jnp.broadcast_to(factor[0:1, 0:1], (PACK, width))
                m[at, cols] = 0.9 * m[at, cols] + 0.1 * one
                v[at, cols] = 0.95 * v[at, cols] + 0.05 * one * one
                return carry

            tiles(b, num, body, 0)

        work.append(compute)

    every = len(copies) / max(len(steps), 1)
    n = 0
    for i, one in enumerate(copies):
        copy_task(*one)
        while n < len(steps) and (n + 0.5) * every <= i + 1:
            moment_task(*steps[n])
            n += 1

    last = {}
    if moments:
        get.wait()
    for i in range(len(users) + DEPTH):
        if i < len(users):
            if users[i] in last:
                for one in stores[last[users[i]]]:
                    one.wait()
            last[users[i]] = i
            for one in loads[i]:
                one.start()
        if 0 <= i - DEPTH < len(users):
            for one in loads[i - DEPTH]:
                one.wait()
            if work[i - DEPTH] is not None:
                work[i - DEPTH]()
            for one in stores[i - DEPTH]:
                one.start()
    for i in last.values():
        for one in stores[i]:
            one.wait()


def settle(done, tmp, passed, moments):
    any_, dma = pl.BlockSpec(memory_space=pl.ANY), pltpu.SemaphoreType.DMA
    operands = [*(tmp[w] for w in done), *passed]
    shapes = [tmp[w] for w in done]
    specs = [any_] * len(operands)
    if moments:
        q, factor, m, v = moments
        operands += [*q, factor, *m, *v]
        specs += [any_] * 10
        shapes += [*m, *v]
    flops = 10**10 * len(done) + (10**10 if moments else 0)
    return pl.pallas_call(
        functools.partial(settle_kernel, done, bool(moments)),
        out_shape=[jax.ShapeDtypeStruct(one.shape, one.dtype) for one in shapes],
        in_specs=specs,
        out_specs=[any_] * len(shapes),
        scratch_shapes=[
            pltpu.VMEM((16, *WIDE), BF), pltpu.VMEM((10, *TALL), BF),
            pltpu.VMEM((5, 2, *HALF_WIDE), FL), pltpu.VMEM((5, 2, *HALF_TALL), FL),
            pltpu.VMEM((5, *HALF_WIDE), BF), pltpu.VMEM((5, *HALF_TALL), BF), pltpu.VMEM(TILE, FL),
            dma((26,)), dma((3, 10) if moments else (1, 1)), dma((1,)),
        ],
        cost_estimate=pl.CostEstimate(flops=flops, bytes_accessed=30 * 10**6, transcendentals=0),
        compiler_params=pltpu.CompilerParams(vmem_limit_bytes=VMEM),
    )(*operands)


def far_kernel(done, arrays, *refs):
    got = refs[len(done):len(done) + 4 * len(arrays)]
    outs, (slots, sem) = dict(zip(done, refs[len(done) + 4 * len(arrays):])), refs[-2:]
    pieces = []
    for i, a in enumerate(arrays):
        for other in HALVES:
            for h in HALVES:
                src = got[4 * i + 2 * other + h]
                for c, row, b, lo, num in passed_on(h):
                    if c == a:
                        pieces.append((src.at[pl.ds(row, num)], rows(outs[BLOCKS[b][0]], b, device_of(3, other), lo, num)))
    stream(pieces, slots, sem, len(pieces))


def far(done, arrays, whole, got):
    any_ = pl.BlockSpec(memory_space=pl.ANY)
    piece, slots = (HALF_WIDE, 20) if 0 in done else (HALF_TALL, 8)
    operands = [*(whole[w] for w in done), *got]
    return pl.pallas_call(
        functools.partial(far_kernel, done, arrays),
        out_shape=[jax.ShapeDtypeStruct(whole[w].shape, BF) for w in done],
        in_specs=[any_] * len(operands),
        out_specs=[any_] * len(done),
        scratch_shapes=[pltpu.VMEM((slots, *piece), BF), pltpu.SemaphoreType.DMA((slots,))],
        input_output_aliases={i: i for i in range(len(done))},
        cost_estimate=pl.CostEstimate(flops=10**8, bytes_accessed=10**6, transcendentals=0),
        compiler_params=pltpu.CompilerParams(vmem_limit_bytes=VMEM),
    )(*operands)


def solution(mesh):
    swap = [[(i, i ^ bit) for i in range(N)] for bit in (4, 2, 1)]

    def move(array, pairs):
        return lax.ppermute(array, "dp", pairs)

    def step(*arrays):
        out = communicate(*arrays)
        tmp, q, factor, ahead, first = out[:3], out[3:6], out[6], (out[7:11], out[11:15]), [out[15:17]]
        for s in (1, 2, 3):
            first.append([move(ahead[h][s], swap[1 - h]) for h in HALVES])
        second = [[move(one, swap[2]) for one in stage] for stage in first]
        got = [[*first[s], *second[s]] for s in range(4)]
        passed = [*ahead[0], *ahead[1]]
        whole = [None] * 3
        whole[0], whole[2], *moments = settle((0, 2), tmp, passed, (q, factor, arrays[6:9], arrays[9:12]))
        (whole[1],) = settle((1,), tmp, passed, None)
        whole[0], whole[1] = far((0, 1), (0, 1), whole, [*got[0], *got[1]])
        (whole[2],) = far((2,), (2,), whole, got[2])
        (whole[2],) = far((2,), (3,), whole, got[3])
        return (*whole, *moments)

    all_of, cut = P(None, None, None), P(None, "dp", None)
    return jax.shard_map(
        step,
        mesh=mesh,
        in_specs=(P(("rep", "dp"), None, None, None),) * 3 + (all_of,) * 3 + (cut,) * 6,
        out_specs=(P("rep", None, None),) * 3 + (P("rep", "dp", None),) * 6,
        check_vma=False,
    )
```

time: 560 us -> 389 us (0.69)
  waiting for transfers between devices: 465 us -> 51.1 us
  Pallas kernels: 0 us -> 329 us
  other arithmetic: 28.7 us -> 0 us
  local copies, waits for them, and re-layouts: 26.8 us -> 0 us
  blocking collectives: 22.2 us -> 0 us
  between operations: 16.8 us -> 0.74 us
  starting transfers between devices: 0.24 us -> 7.69 us
    pallas_call x0 -> x6, Pallas kernels: none -> 329 us  [the longest x1 283 us: communicate(): pl.pallas_call(kernel, out_shape=shapes, in_specs=[any_] * len(arrays), o...]
    reduce_scatter x3 -> x0, waiting for transfers between devices: 264 us -> none  [step(): lax.psum_scatter(t[0], 'dp', scatter_dimension=1, tiled=True)]
    all_gather x3 -> x0, waiting for transfers between devices: 199 us -> none  [step(): whole = [lax.all_gather(one[0], 'dp', axis=1, tiled=True) for one in new]]
    ppermute x0 -> x14, waiting for transfers between devices: none -> 51.1 us  [move(): return lax.ppermute(array, 'dp', pairs)]
    unnamed x17 -> x0, local copies, waits for them, and re-layouts: 26.8 us -> none
    psum x1 -> x0, blocking collectives: 22.2 us -> none  [step(): squares = lax.psum(sum((jnp.sum(g * g) for g in gradients)), 'dp')]
    convert_element_type x3 -> x0, other arithmetic: 20.1 us -> none  [adamw(): return ((w - 0.02 * step).astype(jnp.bfloat16), m, v)]
    reduce_sum x3 -> x0, other arithmetic: 8.63 us -> none  [step(): squares = lax.psum(sum((jnp.sum(g * g) for g in gradients)), 'dp')]
  transfers between devices with their start and end apart: 6 -> 14, of which waited for: 6 -> 2; matrix products, arithmetic and copies ran while one was open for 3% -> 0% of each run, Pallas kernels for 0% -> 11%
where the time goes in v1:
time: 389 us
  Pallas kernels  329 us (85%)
  waiting for transfers between devices  51.1 us (13%)
  starting transfers between devices  7.69 us (2%)
    pallas_call x1, Pallas kernels, communicate(): pl.pallas_call(kernel, out_shape=shapes, in_specs=[any_] * len(arrays), o...  283 us
    ppermute x14, waiting for transfers between devices, move(): return lax.ppermute(array, 'dp', pairs)  51.1 us
    pallas_call x2, Pallas kernels, settle(): pl.pallas_call(functools.partial(settle_kernel, done, bool(moments)), out...  36.4 us
    pallas_call x3, Pallas kernels, far(): pl.pallas_call(functools.partial(far_kernel, done, arrays), out_shape=[ja...  9.85 us
  transfers between devices with their start and end apart: 14, of which 2 were waited for; matrix products, arithmetic and copies ran while one was open for 0% of the time, Pallas kernels for 11%

profile of v1, /device:TPU:0, one launch (start us, length us, event | category | flops | bytes accessed | tf_op | source)
XLA Modules:
  0.0 388.5 jit_solution(2451603822422149606)
XLA Ops:
  0.6 282.7 %shard_map.187 = (bf16[2,1024,3200]{2,1,0:T(8,128)(2,1)}, bf16[2,1024,3200]{2,1,0:T(8,128)(2,1)}, bf16[2,3200,1024]{2,1,0:T(8,128)(2,1)}, bf16[2,128,3200]{2,1,0...) custom-call(bf16[1,2,1024,3200]{3,2,1,0:T(8,128)(2,1)} %gg.1, ...), custom_call_target="tpu_custom_call" | custom-call | tf_op jit(solution)/shard_map/pallas_call | solution.py:386
  283.4 0.8 collective-permute-start.2
  284.1 1.4 collective-permute-start.3
  285.6 0.7 collective-permute-start.6
  286.3 1.2 collective-permute-start.7
  287.5 0.7 collective-permute-start.10
  288.2 45.9 %collective-permute-done.10.refs_1_ = bf16[96,1024]{1,0:T(8,128)(2,1)} collective-permute-done((bf16[96,1024]{1,0:T(8,128)(2,1)}, bf16[96,1024]{1,0:T(8,128)(2,1)}, u32[]{:S(2)}, u32[]{:S(2)}) %collective-permute-start.10) | collective-permute-done | bytes 196640 | tf_op jit(solution)/shard_map/ppermute | solution.py:599
  334.1 0.8 collective-permute-start.11
  335.0 5.2 %collective-permute-done.11.refs_2_ = bf16[96,1024]{1,0:T(8,128)(2,1)} collective-permute-done((bf16[96,1024]{1,0:T(8,128)(2,1)}, bf16[96,1024]{1,0:T(8,128)(2,1)}, u32[]{:S(2)}, u32[]{:S(2)}) %collective-permute-start.11) | collective-permute-done | bytes 196640 | tf_op jit(solution)/shard_map/ppermute | solution.py:599
  340.1 0.0 collective-permute-start.12
  340.1 0.0 collective-permute-done.6.refs_1_
  340.1 0.5 collective-permute-start.8
  340.6 0.0 collective-permute-done.7.refs_2_
  340.6 0.0 collective-permute-start.9
  340.7 0.0 collective-permute-done.2.refs_6_
  340.7 0.5 collective-permute-start.4
  341.2 0.0 collective-permute-done.3.refs_7_
  341.2 0.0 collective-permute-start.5
  341.2 29.1 %shard_map.188 = (bf16[2,1024,3200]{2,1,0:T(8,128)(2,1)}, bf16[2,3200,1024]{2,1,0:T(8,128)(2,1)}, f32[2,128,3200]{2,1,0:T(8,128)}, f32[2,128,3200]{2,1,0:T(8,128...) custom-call(bf16[2,1024,3200]{2,1,0:T(8,128)(2,1)} %get-tuple-element., ...), custom_call_target="tpu_custom_call" | custom-call | flops 30000001024 | bytes 30000000 | tf_op jit(solution)/shard_map/pallas_call | solution.py:549
  370.3 0.0 collective-permute-done.12.refs_3_
  370.3 0.5 collective-permute-start
  370.8 0.0 collective-permute-done.8.refs_3_
  370.8 0.0 collective-permute-start.1
  370.8 0.0 collective-permute-done.9.refs_4_
  370.8 0.5 collective-permute-start.13
  371.3 7.3 %shard_map.189.refs_1_ = bf16[2,1024,3200]{2,1,0:T(8,128)(2,1)} custom-call(bf16[2,1024,3200]{2,1,0:T(8,128)(2,1)} %get-tuple-element.51.refs_0_, bf16[32,3200]{1,0:T(8,128)(2,1)} %get-tuple-element.38.refs_2_.refs_1_, bf16[224,3200]{1,0:T(8,128)(2,1)} %get-tuple-element.39.refs_3_.refs_2_, bf16[304,1024]{1,0:T(8,128)(2,1)} %get-tuple-element.40.refs_4_.refs_3_, ...), custom_call_target="tpu_custom_call" | custom-call | flops 10000000000 | bytes 30000000 | tf_op jit(solution)/shard_map/pallas_call | solution.py:549
  378.6 2.5 shard_map.191.refs_0_
  381.1 0.0 collective-permute-done.13.refs_4_
  381.2 2.0 shard_map.192
  383.1 0.0 collective-permute-done.refs_4_
  383.1 0.0 collective-permute-done.1.refs_5_
  383.2 0.0 collective-permute-done.4.refs_8_
  383.2 0.0 collective-permute-done.5.refs_9_
  383.2 5.4 %shard_map.190 = (bf16[2,1024,3200]{2,1,0:T(8,128)(2,1)}, bf16[2,1024,3200]{2,1,0:T(8,128)(2,1)}) custom-call(bf16[2,1024,3200]{2,1,0:T(8,128)(2,1)} %get-tuple-element.50.refs_0_, bf16[2,1024,3200]{2,1,0:T(8,128)(2,1)} %shard_map.189.refs_1_, bf16[32,3200]{1,0:T(8,128)(2,1)} %get-tuple-element.52.refs_2_, ...), custom_call_target="tpu_custom_call", output_to_operand_aliasing={{0}: (0, {}), {1}: (1, {})} | custom-call | flops 100000000 | bytes 1000000 | tf_op jit(solution)/shard_map/pallas_call | solution.py:583
Async XLA Ops:
  283.4 57.3 %collective-permute-start.2 = (bf16[224,3200]{1,0:T(8,128)(2,1)}, bf16[224,3200]{1,0:T(8,128)(2,1)}, u32[]{:S(2)}, u32[]{:S(2)}) collective-permute-start(bf16[224,3200]{1,0:T(8,128)(2,1)} %get-tuple-element.39.refs_3_.refs_2_), channel_id=1, source_target_pairs={{0,2},{1,3},{2,0},{3,1},{4,6},{5,7},{6,4},{7,5}} | collective-permute-start | bytes 4300808 | tf_op jit(solution)/shard_map/ppermute | solution.py:599
  284.1 57.0 %collective-permute-start.3 = (bf16[224,3200]{1,0:T(8,128)(2,1)}, bf16[224,3200]{1,0:T(8,128)(2,1)}, u32[]{:S(2)}, u32[]{:S(2)}) collective-permute-start(bf16[224,3200]{1,0:T(8,128)(2,1)} %get-tuple-element.43.refs_7_.refs_6_), channel_id=1, source_target_pairs={{0,4},{1,5},{2,6},{3,7},{4,0},{5,1},{6,2},{7,3}} | collective-permute-start | bytes 4300808 | tf_op jit(solution)/shard_map/ppermute | solution.py:599
  285.6 54.6 %collective-permute-start.6 = (bf16[304,1024]{1,0:T(8,128)(2,1)}, bf16[304,1024]{1,0:T(8,128)(2,1)}, u32[]{:S(2)}, u32[]{:S(2)}) collective-permute-start(bf16[304,1024]{1,0:T(8,128)(2,1)} %get-tuple-element.40.refs_4_.refs_3_), channel_id=1, source_target_pairs={{0,2},{1,3},{2,0},{3,1},{4,6},{5,7},{6,4},{7,5}} | collective-permute-start | bytes 1867784 | tf_op jit(solution)/shard_map/ppermute | solution.py:599
  286.3 54.4 %collective-permute-start.7 = (bf16[304,1024]{1,0:T(8,128)(2,1)}, bf16[304,1024]{1,0:T(8,128)(2,1)}, u32[]{:S(2)}, u32[]{:S(2)}) collective-permute-start(bf16[304,1024]{1,0:T(8,128)(2,1)} %get-tuple-element.44.refs_8_.refs_7_), channel_id=1, source_target_pairs={{0,4},{1,5},{2,6},{3,7},{4,0},{5,1},{6,2},{7,3}} | collective-permute-start | bytes 1867784 | tf_op jit(solution)/shard_map/ppermute | solution.py:599
  287.5 46.7 %collective-permute-start.10 = (bf16[96,1024]{1,0:T(8,128)(2,1)}, bf16[96,1024]{1,0:T(8,128)(2,1)}, u32[]{:S(2)}, u32[]{:S(2)}) collective-permute-start(bf16[96,1024]{1,0:T(8,128)(2,1)} %get-tuple-element.41.refs_5_.refs_4_), channel_id=1, source_target_pairs={{0,2},{1,3},{2,0},{3,1},{4,6},{5,7},{6,4},{7,5}} | collective-permute-start | bytes 589832 | tf_op jit(solution)/shard_map/ppermute | solution.py:599
  334.1 6.0 %collective-permute-start.11 = (bf16[96,1024]{1,0:T(8,128)(2,1)}, bf16[96,1024]{1,0:T(8,128)(2,1)}, u32[]{:S(2)}, u32[]{:S(2)}) collective-permute-start(bf16[96,1024]{1,0:T(8,128)(2,1)} %get-tuple-element.45.refs_9_.refs_8_), channel_id=1, source_target_pairs={{0,4},{1,5},{2,6},{3,7},{4,0},{5,1},{6,2},{7,3}} | collective-permute-start | bytes 589832 | tf_op jit(solution)/shard_map/ppermute | solution.py:599
  340.1 30.1 %collective-permute-start.12 = (bf16[96,1024]{1,0:T(8,128)(2,1)}, bf16[96,1024]{1,0:T(8,128)(2,1)}, u32[]{:S(2)}, u32[]{:S(2)}) collective-permute-start(bf16[96,1024]{1,0:T(8,128)(2,1)} %collective-permute-done.10.refs_1_), channel_id=1, source_target_pairs={{0,1},{1,0},{2,3},{3,2},{4,5},{5,4},{6,7},{7,6}} | collective-permute-start | bytes 589832 | tf_op jit(solution)/shard_map/ppermute | solution.py:599
  340.1 30.7 %collective-permute-start.8 = (bf16[304,1024]{1,0:T(8,128)(2,1)}, bf16[304,1024]{1,0:T(8,128)(2,1)}, u32[]{:S(2)}, u32[]{:S(2)}) collective-permute-start(bf16[304,1024]{1,0:T(8,128)(2,1)} %collective-permute-done.6.refs_1_), channel_id=1, source_target_pairs={{0,1},{1,0},{2,3},{3,2},{4,5},{5,4},{6,7},{7,6}} | collective-permute-start | bytes 1867784 | tf_op jit(solution)/shard_map/ppermute | solution.py:599
  340.6 30.2 %collective-permute-start.9 = (bf16[304,1024]{1,0:T(8,128)(2,1)}, bf16[304,1024]{1,0:T(8,128)(2,1)}, u32[]{:S(2)}, u32[]{:S(2)}) collective-permute-start(bf16[304,1024]{1,0:T(8,128)(2,1)} %collective-permute-done.7.refs_2_), channel_id=1, source_target_pairs={{0,1},{1,0},{2,3},{3,2},{4,5},{5,4},{6,7},{7,6}} | collective-permute-start | bytes 1867784 | tf_op jit(solution)/shard_map/ppermute | solution.py:599
  340.7 42.5 %collective-permute-start.4 = (bf16[224,3200]{1,0:T(8,128)(2,1)}, bf16[224,3200]{1,0:T(8,128)(2,1)}, u32[]{:S(2)}, u32[]{:S(2)}) collective-permute-start(bf16[224,3200]{1,0:T(8,128)(2,1)} %collective-permute-done.2.refs_6_), channel_id=1, source_target_pairs={{0,1},{1,0},{2,3},{3,2},{4,5},{5,4},{6,7},{7,6}} | collective-permute-start | bytes 4300808 | tf_op jit(solution)/shard_map/ppermute | solution.py:599
  341.2 42.0 %collective-permute-start.5 = (bf16[224,3200]{1,0:T(8,128)(2,1)}, bf16[224,3200]{1,0:T(8,128)(2,1)}, u32[]{:S(2)}, u32[]{:S(2)}) collective-permute-start(bf16[224,3200]{1,0:T(8,128)(2,1)} %collective-permute-done.3.refs_7_), channel_id=1, source_target_pairs={{0,1},{1,0},{2,3},{3,2},{4,5},{5,4},{6,7},{7,6}} | collective-permute-start | bytes 4300808 | tf_op jit(solution)/shard_map/ppermute | solution.py:599
  370.3 12.9 %collective-permute-start = (bf16[32,3200]{1,0:T(8,128)(2,1)}, bf16[32,3200]{1,0:T(8,128)(2,1)}, u32[]{:S(2)}, u32[]{:S(2)}) collective-permute-start(bf16[32,3200]{1,0:T(8,128)(2,1)} %get-tuple-element.52.refs_2_), channel_id=1, source_target_pairs={{0,1},{1,0},{2,3},{3,2},{4,5},{5,4},{6,7},{7,6}} | collective-permute-start | bytes 614408 | tf_op jit(solution)/shard_map/ppermute | solution.py:599
  370.8 12.4 %collective-permute-start.1 = (bf16[32,3200]{1,0:T(8,128)(2,1)}, bf16[32,3200]{1,0:T(8,128)(2,1)}, u32[]{:S(2)}, u32[]{:S(2)}) collective-permute-start(bf16[32,3200]{1,0:T(8,128)(2,1)} %get-tuple-element.53.refs_3_), channel_id=1, source_target_pairs={{0,1},{1,0},{2,3},{3,2},{4,5},{5,4},{6,7},{7,6}} | collective-permute-start | bytes 614408 | tf_op jit(solution)/shard_map/ppermute | solution.py:599
  370.8 10.3 %collective-permute-start.13 = (bf16[96,1024]{1,0:T(8,128)(2,1)}, bf16[96,1024]{1,0:T(8,128)(2,1)}, u32[]{:S(2)}, u32[]{:S(2)}) collective-permute-start(bf16[96,1024]{1,0:T(8,128)(2,1)} %collective-permute-done.11.refs_2_), channel_id=1, source_target_pairs={{0,1},{1,0},{2,3},{3,2},{4,5},{5,4},{6,7},{7,6}} | collective-permute-start | bytes 589832 | tf_op jit(solution)/shard_map/ppermute | solution.py:599

commit v2 on v1

--- a/solution.py
+++ b/solution.py
@@ -11,8 +11,9 @@
 D, FF, LAYERS, N = 1024, 3200, 2, 8
 COUNT = 3 * LAYERS * D * FF
 BLOCKS = ((0, 0), (0, 1), (1, 0), (1, 1), (2, 0), (2, 1))
-LAST = 96
-FIRST = 32
+NB, DOWN = len(BLOCKS), 4
+LAST = 144
+FIRST = 16
 AHEAD = 6
 RING = 4
 VMEM = 67043328
@@ -26,17 +27,17 @@
 
 
 def rows_of(b):
-    return (WIDE if b < 4 else TALL)[0]
+    return (WIDE if b < DOWN else TALL)[0]
 
 
 def half(b, h):
     rows = rows_of(b)
-    split = rows // 2 if b < 4 else rows // 2 + (8 if b == 4 else -8)
+    split = rows // 2 if b < DOWN else rows // 2 + (8 if b == 4 else -8)
     return (split, rows - split) if h else (0, split)
 
 
 def tiles(b, num, body, carry):
-    full, width = (WIDE[1], 640) if b < 4 else (TALL[1], 512)
+    full, width = (WIDE[1], 640) if b < DOWN else (TALL[1], 512)
 
     def one(i, carry):
         at = pl.ds(pl.multiple_of(i * PACK, PACK), PACK)
@@ -85,16 +86,16 @@
 
     def own(p, r):
         b, _, lo, num = p
-        return own_a.at[b, r, pl.ds(lo, num)] if b < 4 else own_b.at[b - 4, r, pl.ds(lo, num)]
+        return own_a.at[b, r, pl.ds(lo, num)] if b < DOWN else own_b.at[b - DOWN, r, pl.ds(lo, num)]
 
     def part(p, r):
         b, _, lo, num = p
-        return part_a.at[b, r, pl.ds(lo, num)] if b < 4 else part_b.at[b - 4, r, pl.ds(lo, num)]
+        return part_a.at[b, r, pl.ds(lo, num)] if b < DOWN else part_b.at[b - DOWN, r, pl.ds(lo, num)]
 
     def rec(p, k):
         b, h, lo, num = p
         at = pl.ds(lo - half(b, h)[0], num)
-        return rec_a.at[b, h, k, at] if b < 4 else rec_b.at[b - 4, h, k, at]
+        return rec_a.at[b, h, k, at] if b < DOWN else rec_b.at[b - DOWN, h, k, at]
 
     def span(ref, p, dev, lead=()):
         b, _, lo, num = p
@@ -122,17 +123,17 @@
 
     pieces = {}
     for h in HALVES:
-        pieces["S1", h] = [p for b in range(6) for p in (cut(b, h, 16) if b == 0 else cut(b, h))]
-        pieces["S2", h] = [p for b in range(6) for p in cut(b, h)]
-        pieces["R", h] = pieces["G", h] = [p for b in range(6) for p in (cut(b, h, half(b, h)[1] - 48) if b == 5 else cut(b, h))]
+        pieces["S1", h] = [p for b in range(NB) for p in (cut(b, h, 16) if b == 0 else cut(b, h))]
+        pieces["S2", h] = [p for b in range(NB) for p in cut(b, h)]
+        pieces["R", h] = pieces["G", h] = [p for b in range(NB) for p in (cut(b, h, half(b, h)[1] - 48) if b == 5 else cut(b, h))]
     pairs = {kind: list(zip(pieces[kind, 0], pieces[kind, 1], strict=True)) for kind in ("S1", "S2", "R", "G")}
     turns = [("S1", pair) for pair in pairs["S1"]] + [("S2", pair) for pair in pairs["S2"]]
     for n in range(len(pairs["R"]) + 2):
         turns += [("R", pair) for pair in pairs["R"][n:n + 1]] + [("G", pair) for pair in pairs["G"][n - 2:n - 1] if n >= 2]
     units = [(p[0], chip("S1", 0), *p[2:]) for pair in pairs["S1"][:2] for p in pair]
-    units += [(b, chip("S1", 0), 0, rows_of(b)) for b in range(1, 6)]
-    units += [(b, chip("S2", h), 0, rows_of(b)) for b in range(6) for h in HALVES]
-    units += [(b, 0, 0, rows_of(b)) for b in range(6)]
+    units += [(b, chip("S1", 0), 0, rows_of(b)) for b in range(1, NB)]
+    units += [(b, chip("S2", h), 0, rows_of(b)) for b in range(NB) for h in HALVES]
+    units += [(b, 0, 0, rows_of(b)) for b in range(NB)]
     loads, d2ds, here = {}, {}, set()
 
     def fetch_own(i):
@@ -176,7 +177,7 @@
             target[at, cols] = rounded
             return carry + f32(rounded) * f32(rounded) if squares else carry
 
-        width = 640 if b < 4 else 512
+        width = 640 if b < DOWN else 512
         done = tiles(b, num, body, jnp.zeros((PACK, width), FL) if squares else 0)
         if squares:
             sq[...] += fold(done)
@@ -203,7 +204,7 @@
 
     def slot(b, h, lo=0, num=None):
         at = pl.ds(lo, half(b, h)[1] if num is None else num)
-        if b < 4:
+        if b < DOWN:
             return mv_a.at[h, 0, at], mv_a.at[h, 1, at], ws_a.at[h, at]
         return mv_b.at[h, 0, at], mv_b.at[h, 1, at], ws_b.at[h, at]
 
@@ -440,7 +441,7 @@
         get.start()
 
     copies, steps = [], []
-    for b in range(6):
+    for b in range(NB):
         w, _ = BLOCKS[b]
         if moments:
             steps += [(b, h) for h in HALVES]
@@ -471,7 +472,7 @@
         return k % slots
 
     def copy_task(b, src, dst):
-        kind, ref, base = ("wide", wide, 0) if b < 4 else ("tall", tall, wide.shape[0])
+        kind, ref, base = ("wide", wide, 0) if b < DOWN else ("tall", tall, wide.shape[0])
         k = place(kind, ref.shape[0])
         mid = ref.at[k, pl.ds(0, src.shape[0])]
         loads.append([pltpu.make_async_copy(src, mid, c_sem.at[base + k])])
@@ -480,7 +481,7 @@
         users.append((kind, k))
 
     def moment_task(b, h):
-        kind, mv, gs, base = ("a", mv_a, g_a, 0) if b < 4 else ("b", mv_b, g_b, mv_a.shape[0])
+        kind, mv, gs, base = ("a", mv_a, g_a, 0) if b < DOWN else ("b", mv_b, g_b, mv_a.shape[0])
         k = place(kind, mv.shape[0])
         w, layer = BLOCKS[b]
         lo, num = half(b, h)
@@ -571,14 +572,14 @@
             for h in HALVES:
                 src = got[4 * i + 2 * other + h]
                 for c, row, b, lo, num in passed_on(h):
-                    if c == a:
+                    if c == a and BLOCKS[b][0] in done:
                         pieces.append((src.at[pl.ds(row, num)], rows(outs[BLOCKS[b][0]], b, device_of(3, other), lo, num)))
     stream(pieces, slots, sem, len(pieces))
 
 
 def far(done, arrays, whole, got):
     any_ = pl.BlockSpec(memory_space=pl.ANY)
-    piece, slots = (HALF_WIDE, 20) if 0 in done else (HALF_TALL, 8)
+    piece, slots = (HALF_WIDE, 12) if 2 not in done else (HALF_TALL, 8)
     operands = [*(whole[w] for w in done), *got]
     return pl.pallas_call(
         functools.partial(far_kernel, done, arrays),
@@ -609,7 +610,8 @@
         whole = [None] * 3
         whole[0], whole[2], *moments = settle((0, 2), tmp, passed, (q, factor, arrays[6:9], arrays[9:12]))
         (whole[1],) = settle((1,), tmp, passed, None)
-        whole[0], whole[1] = far((0, 1), (0, 1), whole, [*got[0], *got[1]])
+        for w in (0, 1):
+            (whole[w],) = far((w,), (0, 1)[w:], whole, [*got[0], *got[1]][4 * w:])
         (whole[2],) = far((2,), (2,), whole, got[2])
         (whole[2],) = far((2,), (3,), whole, got[3])
         return (*whole, *moments)

time: 389 us -> 385 us (0.990)
    pallas_call x3 -> x4, Pallas kernels: 9.85 us -> 10.2 us  [far(): pl.pallas_call(functools.partial(far_kernel, done, arrays), out_shape=[ja...]
where the time goes in v2:
time: 385 us; the launch traced here: 384 us
  Pallas kernels  327 us (85%)
  waiting for transfers between devices  48.8 us (13%)
  starting transfers between devices  7.51 us (2%)
    pallas_call x1, Pallas kernels, communicate(): pl.pallas_call(kernel, out_shape=shapes, in_specs=[any_] * len(arrays), o...  281 us
    ppermute x14, waiting for transfers between devices, move(): return lax.ppermute(array, 'dp', pairs)  48.8 us
    pallas_call x2, Pallas kernels, settle(): pl.pallas_call(functools.partial(settle_kernel, done, bool(moments)), out...  36.4 us
    pallas_call x4, Pallas kernels, far(): pl.pallas_call(functools.partial(far_kernel, done, arrays), out_shape=[ja...  10.2 us
  transfers between devices with their start and end apart: 14, of which 2 were waited for; matrix products, arithmetic and copies ran while one was open for 0% of the time, Pallas kernels for 11%

profile of v2, /device:TPU:0, one launch (start us, length us, event | category | flops | bytes accessed | tf_op | source)
XLA Modules:
  0.0 384.5 jit_solution(13743725912843251686)
XLA Ops:
  0.6 280.8 %shard_map.187 = (bf16[2,1024,3200]{2,1,0:T(8,128)(2,1)}, bf16[2,1024,3200]{2,1,0:T(8,128)(2,1)}, bf16[2,3200,1024]{2,1,0:T(8,128)(2,1)}, bf16[2,128,3200]{2,1,0...) custom-call(bf16[1,2,1024,3200]{3,2,1,0:T(8,128)(2,1)} %gg.1, ...), custom_call_target="tpu_custom_call" | custom-call | tf_op jit(solution)/shard_map/pallas_call | solution.py:387
  281.5 0.7 collective-permute-start.2
  282.2 1.2 collective-permute-start.3
  283.4 0.8 collective-permute-start.10
  284.2 1.2 collective-permute-start.6
  285.4 0.8 collective-permute-start.7
  286.2 38.4 %collective-permute-done.10.refs_1_ = bf16[144,1024]{1,0:T(8,128)(2,1)} collective-permute-done((bf16[144,1024]{1,0:T(8,128)(2,1)}, bf16[144,1024]{1,0:T(8,128)(2,1)}, u32[]{:S(2)}, u32[]{:S(2)}) %collective-permute-start.10) | collective-permute-done | bytes 294944 | tf_op jit(solution)/shard_map/ppermute | solution.py:600
  324.6 0.7 collective-permute-start.11
  325.3 10.4 %collective-permute-done.11.refs_2_ = bf16[144,1024]{1,0:T(8,128)(2,1)} collective-permute-done((bf16[144,1024]{1,0:T(8,128)(2,1)}, bf16[144,1024]{1,0:T(8,128)(2,1)}, u32[]{:S(2)}, u32[]{:S(2)}) %collective-permute-start.11) | collective-permute-done | bytes 294944 | tf_op jit(solution)/shard_map/ppermute | solution.py:600
  335.7 0.0 collective-permute-start.12
  335.7 0.0 collective-permute-done.6.refs_1_
  335.7 0.5 collective-permute-start.8
  336.2 0.0 collective-permute-done.7.refs_2_
  336.2 0.0 collective-permute-start.9
  336.2 0.0 collective-permute-done.2.refs_5_.refs_1_
  336.2 0.5 collective-permute-start.4
  336.7 0.0 collective-permute-done.3.refs_6_.refs_2_
  336.7 0.0 collective-permute-start.5
  336.7 29.1 %shard_map.188 = (bf16[2,1024,3200]{2,1,0:T(8,128)(2,1)}, bf16[2,3200,1024]{2,1,0:T(8,128)(2,1)}, f32[2,128,3200]{2,1,0:T(8,128)}, f32[2,128,3200]{2,1,0:T(8,128...) custom-call(bf16[2,1024,3200]{2,1,0:T(8,128)(2,1)} %get-tuple-element., ...), custom_call_target="tpu_custom_call" | custom-call | flops 30000001024 | bytes 30000000 | tf_op jit(solution)/shard_map/pallas_call | solution.py:550
  365.8 0.0 collective-permute-done.12.refs_3_
  365.8 0.5 collective-permute-start
  366.3 0.0 collective-permute-done.8.refs_3_
  366.3 0.0 collective-permute-start.1
  366.4 0.0 collective-permute-done.9.refs_4_
  366.4 0.5 collective-permute-start.13
  366.8 7.3 %shard_map.190.refs_0_ = bf16[2,1024,3200]{2,1,0:T(8,128)(2,1)} custom-call(bf16[2,1024,3200]{2,1,0:T(8,128)(2,1)} %get-tuple-element.51.refs_0_, bf16[16,3200]{1,0:T(8,128)(2,1)} %get-tuple-element.36.refs_2_.refs_1_, bf16[240,3200]{1,0:T(8,128)(2,1)} %get-tuple-element.37.refs_3_.refs_2_, bf16[256,1024]{1,0:T(8,128)(2,1)} %get-tuple-element.38.refs_4_.refs_3_, ...), custom_call_target="tpu_custom_call" | custom-call | flops 10000000000 | bytes 30000000 | tf_op jit(solution)/shard_map/pallas_call | solution.py:550
  374.2 2.4 shard_map.192.refs_0_
  376.5 0.0 collective-permute-done.13.refs_4_
  376.6 2.0 shard_map.193
  378.6 0.0 collective-permute-done.4.refs_7_.refs_3_
  378.6 0.0 collective-permute-done.5.refs_8_.refs_4_
  378.6 2.8 shard_map.191
  381.4 0.0 collective-permute-done.refs_3_
  381.4 0.0 collective-permute-done.1.refs_4_
  381.5 3.0 shard_map.189
Async XLA Ops:
  281.5 54.7 %collective-permute-start.2 = (bf16[240,3200]{1,0:T(8,128)(2,1)}, bf16[240,3200]{1,0:T(8,128)(2,1)}, u32[]{:S(2)}, u32[]{:S(2)}) collective-permute-start(bf16[240,3200]{1,0:T(8,128)(2,1)} %get-tuple-element.37.refs_3_.refs_2_), channel_id=1, source_target_pairs={{0,2},{1,3},{2,0},{3,1},{4,6},{5,7},{6,4},{7,5}} | collective-permute-start | bytes 4608008 | tf_op jit(solution)/shard_map/ppermute | solution.py:600
  282.2 54.5 %collective-permute-start.3 = (bf16[240,3200]{1,0:T(8,128)(2,1)}, bf16[240,3200]{1,0:T(8,128)(2,1)}, u32[]{:S(2)}, u32[]{:S(2)}) collective-permute-start(bf16[240,3200]{1,0:T(8,128)(2,1)} %get-tuple-element.41.refs_7_.refs_6_), channel_id=1, source_target_pairs={{0,4},{1,5},{2,6},{3,7},{4,0},{5,1},{6,2},{7,3}} | collective-permute-start | bytes 4608008 | tf_op jit(solution)/shard_map/ppermute | solution.py:600
  283.4 41.2 %collective-permute-start.10 = (bf16[144,1024]{1,0:T(8,128)(2,1)}, bf16[144,1024]{1,0:T(8,128)(2,1)}, u32[]{:S(2)}, u32[]{:S(2)}) collective-permute-start(bf16[144,1024]{1,0:T(8,128)(2,1)} %get-tuple-element.39.refs_5_.refs_4_), channel_id=1, source_target_pairs={{0,2},{1,3},{2,0},{3,1},{4,6},{5,7},{6,4},{7,5}} | collective-permute-start | bytes 884744 | tf_op jit(solution)/shard_map/ppermute | solution.py:600
  284.2 51.5 %collective-permute-start.6 = (bf16[256,1024]{1,0:T(8,128)(2,1)}, bf16[256,1024]{1,0:T(8,128)(2,1)}, u32[]{:S(2)}, u32[]{:S(2)}) collective-permute-start(bf16[256,1024]{1,0:T(8,128)(2,1)} %get-tuple-element.38.refs_4_.refs_3_), channel_id=1, source_target_pairs={{0,2},{1,3},{2,0},{3,1},{4,6},{5,7},{6,4},{7,5}} | collective-permute-start | bytes 1572872 | tf_op jit(solution)/shard_map/ppermute | solution.py:600
  285.4 50.8 %collective-permute-start.7 = (bf16[256,1024]{1,0:T(8,128)(2,1)}, bf16[256,1024]{1,0:T(8,128)(2,1)}, u32[]{:S(2)}, u32[]{:S(2)}) collective-permute-start(bf16[256,1024]{1,0:T(8,128)(2,1)} %get-tuple-element.42.refs_8_.refs_7_), channel_id=1, source_target_pairs={{0,4},{1,5},{2,6},{3,7},{4,0},{5,1},{6,2},{7,3}} | collective-permute-start | bytes 1572872 | tf_op jit(solution)/shard_map/ppermute | solution.py:600
  324.6 11.1 %collective-permute-start.11 = (bf16[144,1024]{1,0:T(8,128)(2,1)}, bf16[144,1024]{1,0:T(8,128)(2,1)}, u32[]{:S(2)}, u32[]{:S(2)}) collective-permute-start(bf16[144,1024]{1,0:T(8,128)(2,1)} %get-tuple-element.43.refs_9_.refs_8_), channel_id=1, source_target_pairs={{0,4},{1,5},{2,6},{3,7},{4,0},{5,1},{6,2},{7,3}} | collective-permute-start | bytes 884744 | tf_op jit(solution)/shard_map/ppermute | solution.py:600
  335.7 30.1 %collective-permute-start.12 = (bf16[144,1024]{1,0:T(8,128)(2,1)}, bf16[144,1024]{1,0:T(8,128)(2,1)}, u32[]{:S(2)}, u32[]{:S(2)}) collective-permute-start(bf16[144,1024]{1,0:T(8,128)(2,1)} %collective-permute-done.10.refs_1_), channel_id=1, source_target_pairs={{0,1},{1,0},{2,3},{3,2},{4,5},{5,4},{6,7},{7,6}} | collective-permute-start | bytes 884744 | tf_op jit(solution)/shard_map/ppermute | solution.py:600
  335.7 30.7 %collective-permute-start.8 = (bf16[256,1024]{1,0:T(8,128)(2,1)}, bf16[256,1024]{1,0:T(8,128)(2,1)}, u32[]{:S(2)}, u32[]{:S(2)}) collective-permute-start(bf16[256,1024]{1,0:T(8,128)(2,1)} %collective-permute-done.6.refs_1_), channel_id=1, source_target_pairs={{0,1},{1,0},{2,3},{3,2},{4,5},{5,4},{6,7},{7,6}} | collective-permute-start | bytes 1572872 | tf_op jit(solution)/shard_map/ppermute | solution.py:600
  336.2 30.2 %collective-permute-start.9 = (bf16[256,1024]{1,0:T(8,128)(2,1)}, bf16[256,1024]{1,0:T(8,128)(2,1)}, u32[]{:S(2)}, u32[]{:S(2)}) collective-permute-start(bf16[256,1024]{1,0:T(8,128)(2,1)} %collective-permute-done.7.refs_2_), channel_id=1, source_target_pairs={{0,1},{1,0},{2,3},{3,2},{4,5},{5,4},{6,7},{7,6}} | collective-permute-start | bytes 1572872 | tf_op jit(solution)/shard_map/ppermute | solution.py:600
  336.2 42.4 %collective-permute-start.4 = (bf16[240,3200]{1,0:T(8,128)(2,1)}, bf16[240,3200]{1,0:T(8,128)(2,1)}, u32[]{:S(2)}, u32[]{:S(2)}) collective-permute-start(bf16[240,3200]{1,0:T(8,128)(2,1)} %collective-permute-done.2.refs_5_.refs_1_), channel_id=1, source_target_pairs={{0,1},{1,0},{2,3},{3,2},{4,5},{5,4},{6,7},{7,6}} | collective-permute-start | bytes 4608008 | tf_op jit(solution)/shard_map/ppermute | solution.py:600
  336.7 41.9 %collective-permute-start.5 = (bf16[240,3200]{1,0:T(8,128)(2,1)}, bf16[240,3200]{1,0:T(8,128)(2,1)}, u32[]{:S(2)}, u32[]{:S(2)}) collective-permute-start(bf16[240,3200]{1,0:T(8,128)(2,1)} %collective-permute-done.3.refs_6_.refs_2_), channel_id=1, source_target_pairs={{0,1},{1,0},{2,3},{3,2},{4,5},{5,4},{6,7},{7,6}} | collective-permute-start | bytes 4608008 | tf_op jit(solution)/shard_map/ppermute | solution.py:600
  365.8 15.6 %collective-permute-start = (bf16[16,3200]{1,0:T(8,128)(2,1)}, bf16[16,3200]{1,0:T(8,128)(2,1)}, u32[]{:S(2)}, u32[]{:S(2)}) collective-permute-start(bf16[16,3200]{1,0:T(8,128)(2,1)} %get-tuple-element.49.refs_1_), channel_id=1, source_target_pairs={{0,1},{1,0},{2,3},{3,2},{4,5},{5,4},{6,7},{7,6}} | collective-permute-start | bytes 307208 | tf_op jit(solution)/shard_map/ppermute | solution.py:600
  366.3 15.1 %collective-permute-start.1 = (bf16[16,3200]{1,0:T(8,128)(2,1)}, bf16[16,3200]{1,0:T(8,128)(2,1)}, u32[]{:S(2)}, u32[]{:S(2)}) collective-permute-start(bf16[16,3200]{1,0:T(8,128)(2,1)} %get-tuple-element.50.refs_2_), channel_id=1, source_target_pairs={{0,1},{1,0},{2,3},{3,2},{4,5},{5,4},{6,7},{7,6}} | collective-permute-start | bytes 307208 | tf_op jit(solution)/shard_map/ppermute | solution.py:600
  366.4 10.2 %collective-permute-start.13 = (bf16[144,1024]{1,0:T(8,128)(2,1)}, bf16[144,1024]{1,0:T(8,128)(2,1)}, u32[]{:S(2)}, u32[]{:S(2)}) collective-permute-start(bf16[144,1024]{1,0:T(8,128)(2,1)} %collective-permute-done.11.refs_2_), channel_id=1, source_target_pairs={{0,1},{1,0},{2,3},{3,2},{4,5},{5,4},{6,7},{7,6}} | collective-permute-start | bytes 884744 | tf_op jit(solution)/shard_map/ppermute | solution.py:600

commit v3 on v2

--- a/solution.py
+++ b/solution.py
@@ -14,8 +14,8 @@
 NB, DOWN = len(BLOCKS), 4
 LAST = 144
 FIRST = 16
-AHEAD = 6
-RING = 4
+AHEAD = 4
+RING = 2
 VMEM = 67043328
 BF, FL = jnp.bfloat16, jnp.float32
 HALVES = (0, 1)
@@ -556,7 +556,7 @@
             pltpu.VMEM((16, *WIDE), BF), pltpu.VMEM((10, *TALL), BF),
             pltpu.VMEM((5, 2, *HALF_WIDE), FL), pltpu.VMEM((5, 2, *HALF_TALL), FL),
             pltpu.VMEM((5, *HALF_WIDE), BF), pltpu.VMEM((5, *HALF_TALL), BF), pltpu.VMEM(TILE, FL),
-            dma((26,)), dma((3, 10) if moments else (1, 1)), dma((1,)),
+            dma((26 if moments else 16,)), dma((3, 10) if moments else (1, 1)), dma((1,)),
         ],
         cost_estimate=pl.CostEstimate(flops=flops, bytes_accessed=30 * 10**6, transcendentals=0),
         compiler_params=pltpu.CompilerParams(vmem_limit_bytes=VMEM),

time: 385 us -> 385 us (level)
  no operation moved by 1% of the time
where the time goes in v3:
time: 385 us; the launch traced here: 384 us
  Pallas kernels  327 us (85%)
  waiting for transfers between devices  48.8 us (13%)
  starting transfers between devices  7.51 us (2%)
    pallas_call x1, Pallas kernels, communicate(): pl.pallas_call(kernel, out_shape=shapes, in_specs=[any_] * len(arrays), o...  281 us
    ppermute x14, waiting for transfers between devices, move(): return lax.ppermute(array, 'dp', pairs)  48.8 us
    pallas_call x2, Pallas kernels, settle(): pl.pallas_call(functools.partial(settle_kernel, done, bool(moments)), out...  36.3 us
    pallas_call x4, Pallas kernels, far(): pl.pallas_call(functools.partial(far_kernel, done, arrays), out_shape=[ja...  10.2 us
  transfers between devices with their start and end apart: 14, of which 2 were waited for; matrix products, arithmetic and copies ran while one was open for 0% of the time, Pallas kernels for 11%

profile of v3, /device:TPU:0, one launch (start us, length us, event | category | flops | bytes accessed | tf_op | source)
XLA Modules:
  0.0 384.3 jit_solution(17472401846043719398)
XLA Ops:
  0.6 280.7 %shard_map.187 = (bf16[2,1024,3200]{2,1,0:T(8,128)(2,1)}, bf16[2,1024,3200]{2,1,0:T(8,128)(2,1)}, bf16[2,3200,1024]{2,1,0:T(8,128)(2,1)}, bf16[2,128,3200]{2,1,0...) custom-call(bf16[1,2,1024,3200]{3,2,1,0:T(8,128)(2,1)} %gg.1, ...), custom_call_target="tpu_custom_call" | custom-call | tf_op jit(solution)/shard_map/pallas_call | solution.py:387
  281.4 0.7 collective-permute-start.2
  282.1 1.2 collective-permute-start.3
  283.3 0.8 collective-permute-start.10
  284.1 1.2 collective-permute-start.6
  285.3 0.8 collective-permute-start.7
  286.2 38.4 %collective-permute-done.10.refs_1_ = bf16[144,1024]{1,0:T(8,128)(2,1)} collective-permute-done((bf16[144,1024]{1,0:T(8,128)(2,1)}, bf16[144,1024]{1,0:T(8,128)(2,1)}, u32[]{:S(2)}, u32[]{:S(2)}) %collective-permute-start.10) | collective-permute-done | bytes 294944 | tf_op jit(solution)/shard_map/ppermute | solution.py:600
  324.5 0.7 collective-permute-start.11
  325.2 10.4 %collective-permute-done.11.refs_2_ = bf16[144,1024]{1,0:T(8,128)(2,1)} collective-permute-done((bf16[144,1024]{1,0:T(8,128)(2,1)}, bf16[144,1024]{1,0:T(8,128)(2,1)}, u32[]{:S(2)}, u32[]{:S(2)}) %collective-permute-start.11) | collective-permute-done | bytes 294944 | tf_op jit(solution)/shard_map/ppermute | solution.py:600
  335.6 0.0 collective-permute-start.12
  335.6 0.0 collective-permute-done.6.refs_1_
  335.6 0.5 collective-permute-start.8
  336.1 0.0 collective-permute-done.7.refs_2_
  336.1 0.0 collective-permute-start.9
  336.1 0.0 collective-permute-done.2.refs_5_.refs_1_
  336.1 0.5 collective-permute-start.4
  336.6 0.0 collective-permute-done.3.refs_6_.refs_2_
  336.6 0.0 collective-permute-start.5
  336.6 29.1 %shard_map.188 = (bf16[2,1024,3200]{2,1,0:T(8,128)(2,1)}, bf16[2,3200,1024]{2,1,0:T(8,128)(2,1)}, f32[2,128,3200]{2,1,0:T(8,128)}, f32[2,128,3200]{2,1,0:T(8,128...) custom-call(bf16[2,1024,3200]{2,1,0:T(8,128)(2,1)} %get-tuple-element., ...), custom_call_target="tpu_custom_call" | custom-call | flops 30000001024 | bytes 30000000 | tf_op jit(solution)/shard_map/pallas_call | solution.py:550
  365.7 0.0 collective-permute-done.12.refs_3_
  365.7 0.5 collective-permute-start
  366.2 0.0 collective-permute-done.8.refs_3_
  366.2 0.0 collective-permute-start.1
  366.3 0.0 collective-permute-done.9.refs_4_
  366.3 0.5 collective-permute-start.13
  366.8 7.2 %shard_map.190.refs_0_ = bf16[2,1024,3200]{2,1,0:T(8,128)(2,1)} custom-call(bf16[2,1024,3200]{2,1,0:T(8,128)(2,1)} %get-tuple-element.51.refs_0_, bf16[16,3200]{1,0:T(8,128)(2,1)} %get-tuple-element.36.refs_2_.refs_1_, bf16[240,3200]{1,0:T(8,128)(2,1)} %get-tuple-element.37.refs_3_.refs_2_, bf16[256,1024]{1,0:T(8,128)(2,1)} %get-tuple-element.38.refs_4_.refs_3_, ...), custom_call_target="tpu_custom_call" | custom-call | flops 10000000000 | bytes 30000000 | tf_op jit(solution)/shard_map/pallas_call | solution.py:550
  374.0 2.4 shard_map.192.refs_0_
  376.4 0.0 collective-permute-done.13.refs_4_
  376.4 2.0 shard_map.193
  378.4 0.0 collective-permute-done.4.refs_7_.refs_3_
  378.5 0.0 collective-permute-done.5.refs_8_.refs_4_
  378.5 2.8 shard_map.191
  381.3 0.0 collective-permute-done.refs_3_
  381.3 0.0 collective-permute-done.1.refs_4_
  381.3 3.0 shard_map.189
Async XLA Ops:
  281.4 54.7 %collective-permute-start.2 = (bf16[240,3200]{1,0:T(8,128)(2,1)}, bf16[240,3200]{1,0:T(8,128)(2,1)}, u32[]{:S(2)}, u32[]{:S(2)}) collective-permute-start(bf16[240,3200]{1,0:T(8,128)(2,1)} %get-tuple-element.37.refs_3_.refs_2_), channel_id=1, source_target_pairs={{0,2},{1,3},{2,0},{3,1},{4,6},{5,7},{6,4},{7,5}} | collective-permute-start | bytes 4608008 | tf_op jit(solution)/shard_map/ppermute | solution.py:600
  282.1 54.5 %collective-permute-start.3 = (bf16[240,3200]{1,0:T(8,128)(2,1)}, bf16[240,3200]{1,0:T(8,128)(2,1)}, u32[]{:S(2)}, u32[]{:S(2)}) collective-permute-start(bf16[240,3200]{1,0:T(8,128)(2,1)} %get-tuple-element.41.refs_7_.refs_6_), channel_id=1, source_target_pairs={{0,4},{1,5},{2,6},{3,7},{4,0},{5,1},{6,2},{7,3}} | collective-permute-start | bytes 4608008 | tf_op jit(solution)/shard_map/ppermute | solution.py:600
  283.3 41.2 %collective-permute-start.10 = (bf16[144,1024]{1,0:T(8,128)(2,1)}, bf16[144,1024]{1,0:T(8,128)(2,1)}, u32[]{:S(2)}, u32[]{:S(2)}) collective-permute-start(bf16[144,1024]{1,0:T(8,128)(2,1)} %get-tuple-element.39.refs_5_.refs_4_), channel_id=1, source_target_pairs={{0,2},{1,3},{2,0},{3,1},{4,6},{5,7},{6,4},{7,5}} | collective-permute-start | bytes 884744 | tf_op jit(solution)/shard_map/ppermute | solution.py:600
  284.1 51.5 %collective-permute-start.6 = (bf16[256,1024]{1,0:T(8,128)(2,1)}, bf16[256,1024]{1,0:T(8,128)(2,1)}, u32[]{:S(2)}, u32[]{:S(2)}) collective-permute-start(bf16[256,1024]{1,0:T(8,128)(2,1)} %get-tuple-element.38.refs_4_.refs_3_), channel_id=1, source_target_pairs={{0,2},{1,3},{2,0},{3,1},{4,6},{5,7},{6,4},{7,5}} | collective-permute-start | bytes 1572872 | tf_op jit(solution)/shard_map/ppermute | solution.py:600
  285.3 50.8 %collective-permute-start.7 = (bf16[256,1024]{1,0:T(8,128)(2,1)}, bf16[256,1024]{1,0:T(8,128)(2,1)}, u32[]{:S(2)}, u32[]{:S(2)}) collective-permute-start(bf16[256,1024]{1,0:T(8,128)(2,1)} %get-tuple-element.42.refs_8_.refs_7_), channel_id=1, source_target_pairs={{0,4},{1,5},{2,6},{3,7},{4,0},{5,1},{6,2},{7,3}} | collective-permute-start | bytes 1572872 | tf_op jit(solution)/shard_map/ppermute | solution.py:600
  324.5 11.1 %collective-permute-start.11 = (bf16[144,1024]{1,0:T(8,128)(2,1)}, bf16[144,1024]{1,0:T(8,128)(2,1)}, u32[]{:S(2)}, u32[]{:S(2)}) collective-permute-start(bf16[144,1024]{1,0:T(8,128)(2,1)} %get-tuple-element.43.refs_9_.refs_8_), channel_id=1, source_target_pairs={{0,4},{1,5},{2,6},{3,7},{4,0},{5,1},{6,2},{7,3}} | collective-permute-start | bytes 884744 | tf_op jit(solution)/shard_map/ppermute | solution.py:600
  335.6 30.1 %collective-permute-start.12 = (bf16[144,1024]{1,0:T(8,128)(2,1)}, bf16[144,1024]{1,0:T(8,128)(2,1)}, u32[]{:S(2)}, u32[]{:S(2)}) collective-permute-start(bf16[144,1024]{1,0:T(8,128)(2,1)} %collective-permute-done.10.refs_1_), channel_id=1, source_target_pairs={{0,1},{1,0},{2,3},{3,2},{4,5},{5,4},{6,7},{7,6}} | collective-permute-start | bytes 884744 | tf_op jit(solution)/shard_map/ppermute | solution.py:600
  335.6 30.7 %collective-permute-start.8 = (bf16[256,1024]{1,0:T(8,128)(2,1)}, bf16[256,1024]{1,0:T(8,128)(2,1)}, u32[]{:S(2)}, u32[]{:S(2)}) collective-permute-start(bf16[256,1024]{1,0:T(8,128)(2,1)} %collective-permute-done.6.refs_1_), channel_id=1, source_target_pairs={{0,1},{1,0},{2,3},{3,2},{4,5},{5,4},{6,7},{7,6}} | collective-permute-start | bytes 1572872 | tf_op jit(solution)/shard_map/ppermute | solution.py:600
  336.1 30.2 %collective-permute-start.9 = (bf16[256,1024]{1,0:T(8,128)(2,1)}, bf16[256,1024]{1,0:T(8,128)(2,1)}, u32[]{:S(2)}, u32[]{:S(2)}) collective-permute-start(bf16[256,1024]{1,0:T(8,128)(2,1)} %collective-permute-done.7.refs_2_), channel_id=1, source_target_pairs={{0,1},{1,0},{2,3},{3,2},{4,5},{5,4},{6,7},{7,6}} | collective-permute-start | bytes 1572872 | tf_op jit(solution)/shard_map/ppermute | solution.py:600
  336.1 42.3 %collective-permute-start.4 = (bf16[240,3200]{1,0:T(8,128)(2,1)}, bf16[240,3200]{1,0:T(8,128)(2,1)}, u32[]{:S(2)}, u32[]{:S(2)}) collective-permute-start(bf16[240,3200]{1,0:T(8,128)(2,1)} %collective-permute-done.2.refs_5_.refs_1_), channel_id=1, source_target_pairs={{0,1},{1,0},{2,3},{3,2},{4,5},{5,4},{6,7},{7,6}} | collective-permute-start | bytes 4608008 | tf_op jit(solution)/shard_map/ppermute | solution.py:600
  336.6 41.8 %collective-permute-start.5 = (bf16[240,3200]{1,0:T(8,128)(2,1)}, bf16[240,3200]{1,0:T(8,128)(2,1)}, u32[]{:S(2)}, u32[]{:S(2)}) collective-permute-start(bf16[240,3200]{1,0:T(8,128)(2,1)} %collective-permute-done.3.refs_6_.refs_2_), channel_id=1, source_target_pairs={{0,1},{1,0},{2,3},{3,2},{4,5},{5,4},{6,7},{7,6}} | collective-permute-start | bytes 4608008 | tf_op jit(solution)/shard_map/ppermute | solution.py:600
  365.7 15.5 %collective-permute-start = (bf16[16,3200]{1,0:T(8,128)(2,1)}, bf16[16,3200]{1,0:T(8,128)(2,1)}, u32[]{:S(2)}, u32[]{:S(2)}) collective-permute-start(bf16[16,3200]{1,0:T(8,128)(2,1)} %get-tuple-element.49.refs_1_), channel_id=1, source_target_pairs={{0,1},{1,0},{2,3},{3,2},{4,5},{5,4},{6,7},{7,6}} | collective-permute-start | bytes 307208 | tf_op jit(solution)/shard_map/ppermute | solution.py:600
  366.2 15.0 %collective-permute-start.1 = (bf16[16,3200]{1,0:T(8,128)(2,1)}, bf16[16,3200]{1,0:T(8,128)(2,1)}, u32[]{:S(2)}, u32[]{:S(2)}) collective-permute-start(bf16[16,3200]{1,0:T(8,128)(2,1)} %get-tuple-element.50.refs_2_), channel_id=1, source_target_pairs={{0,1},{1,0},{2,3},{3,2},{4,5},{5,4},{6,7},{7,6}} | collective-permute-start | bytes 307208 | tf_op jit(solution)/shard_map/ppermute | solution.py:600
  366.3 10.1 %collective-permute-start.13 = (bf16[144,1024]{1,0:T(8,128)(2,1)}, bf16[144,1024]{1,0:T(8,128)(2,1)}, u32[]{:S(2)}, u32[]{:S(2)}) collective-permute-start(bf16[144,1024]{1,0:T(8,128)(2,1)} %collective-permute-done.11.refs_2_), channel_id=1, source_target_pairs={{0,1},{1,0},{2,3},{3,2},{4,5},{5,4},{6,7},{7,6}} | collective-permute-start | bytes 884744 | tf_op jit(solution)/shard_map/ppermute | solution.py:600
